TPU v7x, 32 devices: a whole 2x2x4 slice. The times are simulated.
32 devices in a mesh: graph: 16 (over z, y, x), feat: 2 (over core).
Axes of the slice: x: 2, y: 2, z: 4, core: 2. Of those that a mesh axis runs over, the one named last changes fastest.
Arguments:
- features: bfloat16 [16384, 1024], P('graph', 'feat'), may hold values from -6 to 6
- rel_weight: bfloat16 [8, 1024, 1024], P(None, 'feat'), may hold values from -0.1875 to 0.1875
- self_weight: bfloat16 [1024, 1024], P('feat'), may hold values from -0.1875 to 0.1875
- type_bias: float32 [4, 1024], P(None, 'feat'), may hold values from -3 to 3
- node_type: int32 [16384], P('graph'), may hold values from 0 to 3
- tile_coef: bfloat16 [640, 128, 128], P('graph'), may hold values from -0.375 to 0.375
- tile_source: int32 [16, 40], P('graph'), may hold values from 0 to 23, as said below
- tile_target: int32 [16, 40], P('graph'), may hold values from 0 to 7
- tile_relation: int32 [16, 40], P('graph'), may hold values from 0 to 7
- send_block: int32 [16, 16], P('graph'), may hold values from 0 to 7
- send_live: int32 [16, 16], P('graph'), may hold values from 0 to 1, as said below
Outputs:
- updated: bfloat16 [16384, 1024], P('graph', 'feat')
Inputs may be any that keep to these rules, and one draw needn't show every extreme that they name: send_live[s, s] is 0; partition q receives from 3 to 12 live blocks. `tile_source`: entries below 8 name the partition's own blocks; entry 8 + s names the block received from partition s and stands only where send_live[s, p] is 1; every live received block is named by some tile.
All inputs are finite; a program needn't handle non-finite values.
Results may differ from a plain program's by a relative error of at most 0.0065.
Values may be sent and summed in bfloat16 or wider, within the bound.
A program may use at most 64 MiB of HBM per device.

v0:
```python
import functools

import jax
import jax.numpy as jnp
from jax import lax
from jax.experimental import pallas as pl
from jax.experimental.pallas import tpu as pltpu
from jax.sharding import PartitionSpec as P

MESH = pl.DeviceIdType.MESH
VMEM = 67_043_328


def partner(me, step, count):
    other, bit = 0, 1
    while bit < count:
        other = other + ((me // bit + step // bit) % 2) * bit
        bit *= 2
    return other


def exchange_kernel(
    groups,
    shards,
    block,
    send_block,
    send_live,
    tile_source,
    tile_target,
    tile_relation,
    bias_ref,
    type_ref,
    x_hbm,
    rel_ref,
    self_ref,
    coef_hbm,
    received,
    w_out,
    s_out,
    outgoing,
    x_own,
    x_far,
    w_all,
    h_vmem,
    s_vmem,
    coef,
    products,
    landed,
    send_sem,
    recv_sem,
    pass_send,
    pass_recv,
    side_send,
    side_recv,
    local_sem,
    keep_sem,
):
    me, mine = lax.axis_index("graph"), lax.axis_index("feat")
    blocks, _, width = x_own.shape
    relations = rel_ref.shape[0]
    tiles = coef.shape[0]

    def columns(shard):
        return pl.ds(pl.multiple_of(shard * width, width), width)

    barrier = pltpu.get_barrier_semaphore()

    def greet(step, carry):
        pl.semaphore_signal(
            barrier, inc=1, device_id=(partner(me, step, groups), mine), device_id_type=MESH
        )
        return carry

    lax.fori_loop(1, groups, greet, 0)
    for e in range(1, shards):
        pl.semaphore_signal(
            barrier, inc=1, device_id=(me, (mine + e) % shards), device_id_type=MESH
        )

    x_copy = pltpu.make_async_copy(x_hbm, x_own, local_sem.at[3])
    own_rel = pltpu.make_async_copy(
        rel_ref.at[:, :, columns(mine)], w_all.at[mine, pl.ds(0, relations)], local_sem.at[0]
    )
    own_self = pltpu.make_async_copy(
        self_ref.at[:, columns(mine)], w_all.at[mine, relations], local_sem.at[1]
    )
    coef_copy = pltpu.make_async_copy(coef_hbm, coef, local_sem.at[4])
    x_copy.start()
    own_rel.start()
    own_self.start()
    coef_copy.start()
    x_copy.wait()

    def gather(q, carry):
        picked = x_own[send_block[0, q]].astype(jnp.float32)
        outgoing[q] = (picked * send_live[0, q].astype(jnp.float32)).astype(outgoing.dtype)
        return carry

    lax.fori_loop(0, groups, gather, 0)
    pl.semaphore_wait(barrier, groups - 1 + shards - 1)

    def boundary(step):
        other = partner(me, step, groups)
        return pltpu.make_async_remote_copy(
            src_ref=outgoing.at[other],
            dst_ref=landed.at[me],
            send_sem=send_sem.at[step],
            recv_sem=recv_sem.at[step],
            device_id=(other, mine),
            device_id_type=MESH,
        )

    half = groups // 2
    inner = (me // half + me // max(half // 2, 1)) % 2

    def send(i, carry):
        boundary(1 + (i + inner * (half - 1)) % (groups - 1)).start()
        return carry

    lax.fori_loop(0, groups - 1, send, 0)

    def side(e):
        peer = (mine + e) % shards
        pairs = (
            (x_own, x_far.at[mine]),
            (self_ref.at[:, columns(peer)], w_all.at[mine, relations]),
            (rel_ref.at[:, :, columns(peer)], w_all.at[mine, pl.ds(0, relations)]),
        )
        return [
            pltpu.make_async_remote_copy(
                src_ref=src,
                dst_ref=dst,
                send_sem=side_send.at[e - 1, i],
                recv_sem=side_recv.at[e - 1, i],
                device_id=(me, peer),
                device_id_type=MESH,
            )
            for i, (src, dst) in enumerate(pairs)
        ]

    sides = [copy for e in range(1, shards) for copy in side(e)]
    for copy in sides:
        copy.start()
    own_rel.wait()
    own_self.wait()
    for copy in sides:
        copy.wait()
    w_copy = pltpu.make_async_copy(
        w_all.at[:, pl.ds(0, relations)], w_out, local_sem.at[2]
    )
    w_copy.start()

    chunk = 2

    def full_dot(start, relation):
        at = pl.ds(start, chunk)
        total = jnp.dot(
            x_own[at].reshape(chunk * block, width),
            w_all[mine, relation],
            preferred_element_type=jnp.float32,
        )
        for e in range(1, shards):
            peer = (mine + e) % shards
            total = total + jnp.dot(
                x_far[peer, at].reshape(chunk * block, width),
                w_all[peer, relation],
                preferred_element_type=jnp.float32,
            )
        return total.reshape(chunk, block, width)

    def transform(relation, carry):
        def part(i, inner):
            h_vmem[relation, pl.ds(i * chunk, chunk)] = full_dot(i * chunk, relation).astype(
                h_vmem.dtype
            )
            return inner

        return lax.fori_loop(0, blocks // chunk, part, carry)

    lax.fori_loop(0, relations, transform, 0)

    def own_part(i, carry):
        s_vmem[pl.ds(i * chunk, chunk)] = full_dot(i * chunk, relations)
        return carry

    lax.fori_loop(0, blocks // chunk, own_part, 0)
    for i in range(blocks):
        kinds = jnp.transpose(jnp.broadcast_to(type_ref[i : i + 1, :], (block, block)))
        kinds = jnp.concatenate([kinds] * (width // block), axis=1)
        total = s_vmem[i]
        for kind in range(bias_ref.shape[0]):
            total = total + jnp.where(kinds == kind, bias_ref[kind : kind + 1, :], 0.0)
        s_vmem[i] = total

    coef_copy.wait()
    stride = 4 if tiles % 4 == 0 else 1

    def multiply(i, carry):
        for j in range(stride):
            t = i * stride + j
            source = h_vmem[tile_relation[0, t], jnp.minimum(tile_source[0, t], blocks - 1)]
            products[t] = jnp.dot(coef[t], source, preferred_element_type=jnp.float32)
        return carry

    lax.fori_loop(0, tiles // stride, multiply, 0)
    slab = block // 4

    def accumulate(i, carry):
        target, at = i // 4, pl.ds((i % 4) * slab, slab)

        def step(k, total):
            for j in range(stride):
                t = k * stride + j
                counts = (tile_target[0, t] == target) & (tile_source[0, t] < blocks)
                total = total + products[t, at, :] * jnp.where(counts, 1.0, 0.0)
            return total

        s_vmem[target, at, :] = lax.fori_loop(0, tiles // stride, step, s_vmem[target, at, :])
        return carry

    lax.fori_loop(0, blocks * 4, accumulate, 0)
    s_copy = pltpu.make_async_copy(s_vmem, s_out, local_sem.at[5])

    def forward(step, e):
        other = partner(me, step, groups)
        return pltpu.make_async_remote_copy(
            src_ref=landed.at[other],
            dst_ref=received.at[mine, other],
            send_sem=pass_send.at[e - 1, step],
            recv_sem=pass_recv.at[e - 1, step],
            device_id=(me, (mine + e) % shards),
            device_id_type=MESH,
        )

    def keep(step):
        other = partner(me, step, groups)
        return pltpu.make_async_copy(
            landed.at[other], received.at[mine, other], keep_sem.at[step]
        )

    quarter = max(groups // 4, 1)

    def arrived(i, carry):
        turn = i // quarter
        step = ((turn % 2) * 2 + (turn // 2 + inner) % 2) * quarter + i % quarter

        @pl.when(step > 0)
        def _():
            boundary(step).wait_recv()
            keep(step).start()
            for e in range(1, shards):
                forward(step, e).start()

        return carry

    lax.fori_loop(0, groups - 1, arrived, 0)
    s_copy.start()
    lax.fori_loop(groups - 1, groups, arrived, 0)

    def finish(step, carry):
        boundary(step).wait_send()
        keep(step).wait()
        for e in range(1, shards):
            forward(step, e).wait_send()
            origin = (mine + shards - e) % shards
            other = partner(me, step, groups)
            pltpu.make_async_remote_copy(
                src_ref=received.at[origin, other],
                dst_ref=received.at[origin, other],
                send_sem=pass_send.at[e - 1, step],
                recv_sem=pass_recv.at[e - 1, step],
                device_id=(me, (mine + e) % shards),
                device_id_type=MESH,
            ).wait_recv()
        return carry

    lax.fori_loop(1, groups, finish, 0)
    w_copy.wait()
    s_copy.wait()


def tile_kernel(
    tile_source,
    tile_target,
    tile_relation,
    coef_hbm,
    s_hbm,
    received,
    w_hbm,
    out_hbm,
    coef,
    x_tiles,
    w_vmem,
    total,
    result,
    w_state,
    chosen,
    tile_sem,
    coef_sem,
    w_sem,
    base_sem,
):
    tiles = coef.shape[0]
    shards = w_vmem.shape[1]
    own = result.shape[0]

    total_copy = pltpu.make_async_copy(s_hbm, total.at[pl.ds(0, own)], base_sem.at[0])
    total_copy.start()

    def source_copy(j, t):
        return pltpu.make_async_copy(
            received.at[:, tile_source[0, t] - own], x_tiles.at[j], tile_sem.at[j]
        )

    def coef_copy(j, t):
        return pltpu.make_async_copy(coef_hbm.at[t], coef.at[j], coef_sem.at[j])

    def w_copy(r):
        return pltpu.make_async_copy(w_hbm.at[:, r], w_vmem.at[r], w_sem.at[r])

    for r in range(w_vmem.shape[0]):
        w_state[r] = 0

    def start(t, count):
        relation = tile_relation[0, t]
        is_remote = tile_source[0, t] >= own

        @pl.when(is_remote)
        def _():
            chosen[count] = t
            source_copy(count, t).start()

            @pl.when(w_state[relation] == 0)
            def _():
                w_copy(relation).start()
                w_state[relation] = 1

            coef_copy(count, t).start()

        return count + is_remote.astype(jnp.int32)

    count = lax.fori_loop(0, tiles, start, 0)
    total_copy.wait()

    def ready(j):
        t = chosen[j]
        relation = tile_relation[0, t]

        @pl.when(w_state[relation] == 1)
        def _():
            w_copy(relation).wait()
            w_state[relation] = 2

        source_copy(j, t).wait()
        coef_copy(j, t).wait()

    def moved(j, relation):
        value = jnp.dot(x_tiles[j, 0], w_vmem[relation, 0], preferred_element_type=jnp.float32)
        for e in range(1, shards):
            value = value + jnp.dot(
                x_tiles[j, e], w_vmem[relation, e], preferred_element_type=jnp.float32
            )
        value = value.astype(coef.dtype)
        return jnp.dot(coef[j], value, preferred_element_type=jnp.float32)

    lanes = 4

    def several(i, carry):
        parts = []
        for k in range(lanes):
            j = lanes * i + k
            present = j < count

            @pl.when(present)
            def _(j=j):
                ready(j)

            parts.append((jnp.where(present, j, lanes * i), present))
        sums = []
        for j, present in parts:
            t = chosen[j]
            at = jnp.where(present, tile_target[0, t], own)
            sums.append((at, moved(j, tile_relation[0, t])))
        for at, value in sums:
            total[at] += value
        return carry

    lax.fori_loop(0, (count + lanes - 1) // lanes, several, 0)
    outs = []
    for i in range(own):
        result[i] = jnp.maximum(total[i], 0.0).astype(result.dtype)
        outs.append(pltpu.make_async_copy(result.at[i], out_hbm.at[i], base_sem.at[1 + i]))
        if i > 0:
            outs[i - 1].start()
    outs[-1].start()
    for copy in outs:
        copy.wait()


def per_device(
    groups,
    shards,
    features,
    rel_weight,
    self_weight,
    type_bias,
    node_type,
    tile_coef,
    tile_source,
    tile_target,
    tile_relation,
    send_block,
    send_live,
):
    rows, width = features.shape
    tiles, block, _ = tile_coef.shape
    relations = rel_weight.shape[0]
    kind = features.dtype
    smem = pl.BlockSpec(memory_space=pltpu.SMEM)
    vmem = pl.BlockSpec(memory_space=pltpu.VMEM)
    anywhere = pl.BlockSpec(memory_space=pl.ANY)
    dma = pltpu.SemaphoreType.DMA
    blocks = rows // block
    received, weights, base = pl.pallas_call(
        functools.partial(exchange_kernel, groups, shards, block),
        out_shape=(
            jax.ShapeDtypeStruct((shards, groups, block, width), kind),
            jax.ShapeDtypeStruct((shards, relations, width, width), kind),
            jax.ShapeDtypeStruct((blocks, block, width), jnp.float32),
        ),
        in_specs=[smem] * 5 + [vmem] * 2 + [anywhere] * 4,
        out_specs=(anywhere,) * 3,
        scratch_shapes=[
            pltpu.VMEM((groups, block, width), kind),
            pltpu.VMEM((blocks, block, width), kind),
            pltpu.VMEM((shards, blocks, block, width), kind),
            pltpu.VMEM((shards, relations + 1, width, width), kind),
            pltpu.VMEM((relations, blocks, block, width), kind),
            pltpu.VMEM((blocks, block, width), jnp.float32),
            pltpu.VMEM((tiles, block, block), kind),
            pltpu.VMEM((tiles, block, width), jnp.float32),
            pltpu.VMEM((groups, block, width), kind),
            dma((groups,)),
            dma((groups,)),
            dma((max(shards - 1, 1), groups)),
            dma((max(shards - 1, 1), groups)),
            dma((max(shards - 1, 1), 3)),
            dma((max(shards - 1, 1), 3)),
            dma((6,)),
            dma((groups,)),
        ],
        compiler_params=pltpu.CompilerParams(
            collective_id=0, has_side_effects=True, vmem_limit_bytes=VMEM
        ),
        name="exchange",
    )(
        send_block,
        send_live,
        tile_source,
        tile_target,
        tile_relation,
        type_bias,
        node_type.reshape(blocks, block),
        features.reshape(blocks, block, width),
        rel_weight,
        self_weight,
        tile_coef,
    )
    updated = pl.pallas_call(
        tile_kernel,
        out_shape=jax.ShapeDtypeStruct((blocks, block, width), kind),
        in_specs=[smem] * 3 + [anywhere] * 4,
        out_specs=anywhere,
        scratch_shapes=[
            pltpu.VMEM((tiles, block, block), kind),
            pltpu.VMEM((tiles, shards, block, width), kind),
            pltpu.VMEM((relations, shards, width, width), kind),
            pltpu.VMEM((blocks + 1, block, width), jnp.float32),
            pltpu.VMEM((blocks, block, width), kind),
            pltpu.SMEM((relations,), jnp.int32),
            pltpu.SMEM((tiles,), jnp.int32),
            dma((tiles,)),
            dma((tiles,)),
            dma((relations,)),
            dma((1 + blocks,)),
        ],
        compiler_params=pltpu.CompilerParams(vmem_limit_bytes=VMEM),
        name="tiles",
    )(tile_source, tile_target, tile_relation, tile_coef, base, received, weights)
    return updated.reshape(rows, width)


def solution(mesh):
    placed = (
        P("graph", "feat"),
        P(None, "feat", None),
        P("feat", None),
        P(None, "feat"),
        P("graph"),
        P("graph", None, None),
        P("graph", None),
        P("graph", None),
        P("graph", None),
        P("graph", None),
        P("graph", None),
    )
    groups, shards = mesh.shape["graph"], mesh.shape["feat"]
    return jax.shard_map(
        functools.partial(per_device, groups, shards),
        mesh=mesh,
        in_specs=placed,
        out_specs=P("graph", "feat"),
        check_vma=False,
    )
```

profile of v0, /device:TPU:23, one launch (start us, length us, event | category | flops | bytes accessed | tf_op | source)
XLA Modules:
  0.0 65.3 jit_solution(18423304081975525225)
XLA Ops:
  0.0 55.2 %exchange.1 = (bf16[2,16,128,512]{3,2,1,0:T(8,128)(2,1)}, bf16[2,8,512,512]{3,2,1,0:T(8,128)(2,1)}, f32[8,128,512]{2,1,0:T(8,128)}) custom-call(s32[1,16]{1,0:T(1,128)} %send_block.1, s32[1,16]{1,0:T(1,128)} %send_live.1, s32[1,40]{1,0:T(1,128)} %tile_source.3, s32[1,40]{1,0:T(1,128)} %tile_target.3, s32[1,40]{1,0:T(1,128)} %tile_relation.3, ...), custom_call_target="tpu_custom_call" | custom-call | tf_op jit(solution)/shard_map/exchange/pallas_call | solution.py:424
  55.2 10.0 %tiles.1 = bf16[8,128,512]{2,1,0:T(8,128)(2,1)} custom-call(s32[1,40]{1,0:T(1,128)} %tile_source.3, s32[1,40]{1,0:T(1,128)} %tile_target.3, s32[1,40]{1,0:T(1,128)} %tile_relation.3, bf16[40,128,128]{2,1,0:T(8,128)(2,1)} %coef_hbm.3, f32[8,128,512]{2,1,0:T(8,128)} %get-tuple-element.8.s_hbm, bf16[2,16,128,512]{3,2,1,0:T(8,128)(2,1)} %get-tuple-element.9.received, ...), custom_call_target="tpu_custom_call" | custom-call | tf_op jit(solution)/shard_map/tiles/pallas_call | solution.py:469
where the time goes:
time: 65.5 us; the launch traced here: 65.3 us
  Pallas kernels  65.3 us (100%)
    pallas_call x1, Pallas kernels, per_device(): pl.pallas_call(functools.partial(exchange_kernel, groups, shards, block),...  55.2 us
    pallas_call x1, Pallas kernels, per_device(): pl.pallas_call(tile_kernel, out_shape=jax.ShapeDtypeStruct((blocks, block...  10 us

commit v1 on v0

v1 whole, which is shorter than its diff:
```python
import functools

import jax
import jax.numpy as jnp
from jax import lax
from jax.experimental import pallas as pl
from jax.experimental.pallas import tpu as pltpu
from jax.sharding import PartitionSpec as P

MESH = pl.DeviceIdType.MESH
VMEM = 67_043_328


def partner(me, step, count):
    other, bit = 0, 1
    while bit < count:
        other = other + ((me // bit + step // bit) % 2) * bit
        bit *= 2
    return other


def exchange_kernel(
    groups,
    shards,
    block,
    send_block,
    send_live,
    tile_source,
    tile_target,
    tile_relation,
    source_row,
    target_row,
    bias_ref,
    type_ref,
    x_hbm,
    rel_ref,
    self_ref,
    coef_hbm,
    received,
    w_out,
    pre_out,
    outgoing,
    x_own,
    x_far,
    w_all,
    s_vmem,
    coef,
    sums,
    landed,
    far,
    pre,
    plan_vmem,
    plan,
    send_sem,
    recv_sem,
    pass_send,
    pass_recv,
    side_send,
    side_recv,
    local_sem,
    keep_sem,
    far_sem,
    out_sem,
):
    me, mine = lax.axis_index("graph"), lax.axis_index("feat")
    blocks, _, width = x_own.shape
    relations = rel_ref.shape[0]
    tiles = coef.shape[0]

    def columns(shard):
        return pl.ds(pl.multiple_of(shard * width, width), width)

    barrier = pltpu.get_barrier_semaphore()

    def greet(step, carry):
        pl.semaphore_signal(
            barrier, inc=1, device_id=(partner(me, step, groups), mine), device_id_type=MESH
        )
        return carry

    lax.fori_loop(1, groups, greet, 0)
    for e in range(1, shards):
        pl.semaphore_signal(
            barrier, inc=1, device_id=(me, (mine + e) % shards), device_id_type=MESH
        )

    x_copy = pltpu.make_async_copy(x_hbm, x_own, local_sem.at[3])
    own_rel = pltpu.make_async_copy(
        rel_ref.at[:, :, columns(mine)], w_all.at[mine, pl.ds(0, relations)], local_sem.at[0]
    )
    own_self = pltpu.make_async_copy(
        self_ref.at[:, columns(mine)], w_all.at[mine, relations], local_sem.at[1]
    )
    coef_copy = pltpu.make_async_copy(coef_hbm, coef, local_sem.at[4])
    x_copy.start()
    own_rel.start()
    own_self.start()
    coef_copy.start()
    x_copy.wait()

    def gather(q, carry):
        picked = x_own[send_block[0, q]].astype(jnp.float32)
        outgoing[q] = (picked * send_live[0, q].astype(jnp.float32)).astype(outgoing.dtype)
        return carry

    lax.fori_loop(0, groups, gather, 0)

    def iota(shape, axis):
        return lax.broadcasted_iota(jnp.int32, shape, axis)

    square = (tiles, tiles)
    down, along = iota(square, 0), iota(square, 1)

    def column(row):
        return jnp.sum(
            jnp.where(down == along, jnp.broadcast_to(row, square), 0), axis=1, keepdims=True
        )

    sources = column(source_row[...])
    keys_row = jnp.where(source_row[...] < blocks, target_row[...], blocks)
    keys = column(keys_row)
    ahead = (keys_row < keys) | ((keys_row == keys) & (along < down))
    rank = jnp.sum(ahead.astype(jnp.int32), axis=1, keepdims=True)
    plan_vmem[0:1, 0:tiles] = jnp.sum(
        jnp.where(rank == along, down, 0), axis=0, keepdims=True
    )
    wide = (tiles, groups)
    plan_vmem[1:2, 0:groups] = jnp.min(
        jnp.where(sources == blocks + iota(wide, 1), iota(wide, 0), tiles), axis=0, keepdims=True
    )
    each = (tiles, blocks)
    plan_vmem[2:3, 0:blocks] = jnp.sum(
        (keys <= iota(each, 1)).astype(jnp.int32), axis=0, keepdims=True
    )
    plan_vmem[3:4, 0:blocks] = jnp.sum(
        (keys == iota(each, 1)).astype(jnp.int32), axis=0, keepdims=True
    )
    plan_copy = pltpu.make_async_copy(plan_vmem, plan, local_sem.at[5])
    with jax.named_scope("barrier"):
        pl.semaphore_wait(barrier, groups - 1 + shards - 1)

    def boundary(step):
        other = partner(me, step, groups)
        return pltpu.make_async_remote_copy(
            src_ref=outgoing.at[other],
            dst_ref=landed.at[me],
            send_sem=send_sem.at[step],
            recv_sem=recv_sem.at[step],
            device_id=(other, mine),
            device_id_type=MESH,
        )

    half = groups // 2
    inner = (me // half + me // max(half // 2, 1)) % 2

    def send(i, carry):
        boundary(1 + (i + inner * (half - 1)) % (groups - 1)).start()
        return carry

    lax.fori_loop(0, groups - 1, send, 0)
    plan_copy.start()

    def side(e):
        peer = (mine + e) % shards
        pairs = (
            (x_own, x_far.at[mine]),
            (self_ref.at[:, columns(peer)], w_all.at[mine, relations]),
            (rel_ref.at[:, :, columns(peer)], w_all.at[mine, pl.ds(0, relations)]),
        )
        return [
            pltpu.make_async_remote_copy(
                src_ref=src,
                dst_ref=dst,
                send_sem=side_send.at[e - 1, i],
                recv_sem=side_recv.at[e - 1, i],
                device_id=(me, peer),
                device_id_type=MESH,
            )
            for i, (src, dst) in enumerate(pairs)
        ]

    sides = [copy for e in range(1, shards) for copy in side(e)]
    for copy in sides:
        copy.start()
    own_rel.wait()
    own_self.wait()
    with jax.named_scope("sides"):
        for copy in sides:
            copy.wait()
    w_copy = pltpu.make_async_copy(
        w_all.at[:, pl.ds(0, relations)], w_out, local_sem.at[2]
    )
    w_copy.start()

    chunk = 2

    def full_dot(start, relation):
        at = pl.ds(start, chunk)
        total = jnp.dot(
            x_own[at].reshape(chunk * block, width),
            w_all[mine, relation],
            preferred_element_type=jnp.float32,
        )
        for e in range(1, shards):
            peer = (mine + e) % shards
            total = total + jnp.dot(
                x_far[peer, at].reshape(chunk * block, width),
                w_all[peer, relation],
                preferred_element_type=jnp.float32,
            )
        return total.reshape(chunk, block, width)

    def own_part(i, carry):
        s_vmem[pl.ds(i * chunk, chunk)] = full_dot(i * chunk, relations)
        return carry

    with jax.named_scope("self"):
        lax.fori_loop(0, blocks // chunk, own_part, 0)

    coef_copy.wait()
    plan_copy.wait()
    stride = 4 if tiles % 4 == 0 else 1

    def local(i, carry):
        terms = []
        for j in range(stride):
            t = plan[0, i * stride + j]
            relation = tile_relation[0, t]
            source = jnp.minimum(tile_source[0, t], blocks - 1)
            value = jnp.dot(
                x_own[source], w_all[mine, relation], preferred_element_type=jnp.float32
            )
            for e in range(1, shards):
                peer = (mine + e) % shards
                value = value + jnp.dot(
                    x_far[peer, source], w_all[peer, relation], preferred_element_type=jnp.float32
                )
            terms.append((t, value.astype(coef.dtype)))
        for j, (t, value) in enumerate(terms):
            at = i * stride + j
            before = plan[0, jnp.maximum(at - 1, 0)]
            joins = (tile_target[0, t] == tile_target[0, before]) & (at > 0)
            term = jnp.dot(coef[t], value, preferred_element_type=jnp.float32)
            sums[at] = term + jnp.where(joins, sums[jnp.maximum(at - 1, 0)], 0.0)
        return carry

    with jax.named_scope("local"):
        lax.fori_loop(0, tiles // stride, local, 0)

    with jax.named_scope("base"):
        for i in range(blocks):
            kinds = jnp.transpose(jnp.broadcast_to(type_ref[i : i + 1, :], (block, block)))
            kinds = jnp.concatenate([kinds] * (width // block), axis=1)
            total = s_vmem[i]
            for kind in range(bias_ref.shape[0]):
                total = total + jnp.where(kinds == kind, bias_ref[kind : kind + 1, :], 0.0)
            last = jnp.maximum(plan[2, i] - 1, 0)
            s_vmem[i] = total + jnp.where(plan[3, i] > 0, sums[last], 0.0)

    def forward(step, e):
        other = partner(me, step, groups)
        return pltpu.make_async_remote_copy(
            src_ref=landed.at[other],
            dst_ref=far.at[mine, other],
            send_sem=pass_send.at[e - 1, step],
            recv_sem=pass_recv.at[e - 1, step],
            device_id=(me, (mine + e) % shards),
            device_id_type=MESH,
        )

    def keep(step):
        other = partner(me, step, groups)
        return pltpu.make_async_copy(
            landed.at[other], received.at[mine, other], keep_sem.at[step]
        )

    def keep_far(step, e):
        origin, other = (mine + shards - e) % shards, partner(me, step, groups)
        return pltpu.make_async_copy(
            far.at[origin, other], received.at[origin, other], far_sem.at[e - 1, step]
        )

    def arrived(step, carry):
        boundary(step).wait_recv()
        for e in range(1, shards):
            forward(step, e).start()
        keep(step).start()
        return carry

    def moved(step):
        other = partner(me, step, groups)
        found = plan[1, other]
        t = jnp.minimum(found, tiles - 1)
        relation = tile_relation[0, t]
        value = jnp.dot(
            landed[other], w_all[mine, relation], preferred_element_type=jnp.float32
        )
        for e in range(1, shards):
            origin = (mine + shards - e) % shards
            pltpu.make_async_remote_copy(
                src_ref=far.at[origin, other],
                dst_ref=far.at[origin, other],
                send_sem=pass_send.at[e - 1, step],
                recv_sem=pass_recv.at[e - 1, step],
                device_id=(me, (mine + e) % shards),
                device_id_type=MESH,
            ).wait_recv()
            keep_far(step, e).start()
            value = value + jnp.dot(
                far[origin, other], w_all[origin, relation], preferred_element_type=jnp.float32
            )
        value = value.astype(coef.dtype)
        result = jnp.dot(coef[t], value, preferred_element_type=jnp.float32)
        return result, jnp.where(found < tiles, tile_target[0, t], -1)

    def merge(step, carry):
        result, target = moved(step)
        for i in range(blocks):
            s_vmem[i] = s_vmem[i] + jnp.where(target == i, result, 0.0)
        return carry

    late = max(groups // 4, 1)

    def serve(step, carry):
        arrived(step, carry)
        return merge(step, carry)

    with jax.named_scope("arrive"):
        lax.fori_loop(1, groups - late, arrived, 0)
    with jax.named_scope("merge"):
        lax.fori_loop(1, groups - late, merge, 0)
    with jax.named_scope("serve"):
        lax.fori_loop(max(groups - late, 1), groups - 1, serve, 0)
    with jax.named_scope("last"):
        arrived(groups - 1, 0)
    with jax.named_scope("lastmv"):
        result, target = moved(groups - 1)
        outs = []
        for i in range(blocks):
            pre[i] = (s_vmem[i] + jnp.where(target == i, result, 0.0)).astype(pre.dtype)
            outs.append(pltpu.make_async_copy(pre.at[i], pre_out.at[i], out_sem.at[i]))
            if i > 0:
                outs[i - 1].start()
        outs[-1].start()

    def finish(step, carry):
        boundary(step).wait_send()
        keep(step).wait()
        for e in range(1, shards):
            forward(step, e).wait_send()
            keep_far(step, e).wait()
        return carry

    with jax.named_scope("finish"):
        lax.fori_loop(1, groups, finish, 0)
        w_copy.wait()
        for copy in outs:
            copy.wait()


def tile_kernel(
    tile_source,
    tile_target,
    tile_relation,
    coef_hbm,
    pre_hbm,
    received,
    w_hbm,
    out_hbm,
    coef,
    x_tiles,
    w_vmem,
    total,
    pre,
    result,
    seen,
    sems,
):
    tiles = tile_source.shape[1]
    shards, groups = received.shape[:2]
    own = result.shape[0]
    ins = [pltpu.make_async_copy(pre_hbm.at[i], pre.at[i], sems.at[i]) for i in range(own)]
    outs = [
        pltpu.make_async_copy(result.at[i], out_hbm.at[i], sems.at[own + i]) for i in range(own)
    ]
    for copy in ins:
        copy.start()
    for s in range(groups):
        seen[s] = 0

    def look(t, count):
        source = tile_source[0, t] - own

        def repeated():
            before = seen[source]
            seen[source] = 1
            return count + before

        return lax.cond(source >= 0, repeated, lambda: count)

    count = lax.fori_loop(0, tiles, look, 0)

    @pl.when(count == 0)
    def _():
        for i in range(own):
            ins[i].wait()
            result[i] = jnp.maximum(pre[i].astype(jnp.float32), 0.0).astype(result.dtype)
            if i > 0:
                outs[i - 1].start()

    @pl.when(count > 0)
    def _():
        for i in range(own):
            ins[i].wait()
            total[i] = pre[i].astype(jnp.float32)
        for s in range(groups):
            seen[s] = 0

        def add(t, carry):
            source = tile_source[0, t] - own

            @pl.when(source >= 0)
            def _():
                before = seen[source]
                seen[source] = 1

                @pl.when(before == 1)
                def _():
                    copies = [
                        pltpu.make_async_copy(received.at[:, source], x_tiles, sems.at[2 * own]),
                        pltpu.make_async_copy(
                            w_hbm.at[:, tile_relation[0, t]], w_vmem, sems.at[2 * own + 1]
                        ),
                        pltpu.make_async_copy(coef_hbm.at[t], coef, sems.at[2 * own + 2]),
                    ]
                    for copy in copies:
                        copy.start()
                    for copy in copies:
                        copy.wait()
                    value = jnp.dot(x_tiles[0], w_vmem[0], preferred_element_type=jnp.float32)
                    for e in range(1, shards):
                        value = value + jnp.dot(
                            x_tiles[e], w_vmem[e], preferred_element_type=jnp.float32
                        )
                    total[tile_target[0, t]] += jnp.dot(
                        coef[...], value.astype(coef.dtype), preferred_element_type=jnp.float32
                    )

            return carry

        lax.fori_loop(0, tiles, add, 0)
        for i in range(own):
            result[i] = jnp.maximum(total[i], 0.0).astype(result.dtype)
            if i > 0:
                outs[i - 1].start()

    outs[-1].start()
    for copy in outs:
        copy.wait()


def per_device(
    groups,
    shards,
    features,
    rel_weight,
    self_weight,
    type_bias,
    node_type,
    tile_coef,
    tile_source,
    tile_target,
    tile_relation,
    send_block,
    send_live,
):
    rows, width = features.shape
    tiles, block, _ = tile_coef.shape
    relations = rel_weight.shape[0]
    kind = features.dtype
    smem = pl.BlockSpec(memory_space=pltpu.SMEM)
    vmem = pl.BlockSpec(memory_space=pltpu.VMEM)
    anywhere = pl.BlockSpec(memory_space=pl.ANY)
    dma = pltpu.SemaphoreType.DMA
    blocks = rows // block
    lanes = 128 * pl.cdiv(max(tiles, groups, blocks), 128)
    received, weights, pre = pl.pallas_call(
        functools.partial(exchange_kernel, groups, shards, block),
        out_shape=(
            jax.ShapeDtypeStruct((shards, groups, block, width), kind),
            jax.ShapeDtypeStruct((shards, relations, width, width), kind),
            jax.ShapeDtypeStruct((blocks, block, width), kind),
        ),
        in_specs=[smem] * 5 + [vmem] * 4 + [anywhere] * 4,
        out_specs=(anywhere,) * 3,
        scratch_shapes=[
            pltpu.VMEM((groups, block, width), kind),
            pltpu.VMEM((blocks, block, width), kind),
            pltpu.VMEM((shards, blocks, block, width), kind),
            pltpu.VMEM((shards, relations + 1, width, width), kind),
            pltpu.VMEM((blocks, block, width), jnp.float32),
            pltpu.VMEM((tiles, block, block), kind),
            pltpu.VMEM((tiles, block, width), jnp.float32),
            pltpu.VMEM((groups, block, width), kind),
            pltpu.VMEM((shards, groups, block, width), kind),
            pltpu.VMEM((blocks, block, width), kind),
            pltpu.VMEM((8, lanes), jnp.int32),
            pltpu.SMEM((8, lanes), jnp.int32),
            dma((groups,)),
            dma((groups,)),
            dma((max(shards - 1, 1), groups)),
            dma((max(shards - 1, 1), groups)),
            dma((max(shards - 1, 1), 3)),
            dma((max(shards - 1, 1), 3)),
            dma((6,)),
            dma((groups,)),
            dma((max(shards - 1, 1), groups)),
            dma((blocks,)),
        ],
        compiler_params=pltpu.CompilerParams(
            collective_id=0, has_side_effects=True, vmem_limit_bytes=VMEM
        ),
        name="exchange",
    )(
        send_block,
        send_live,
        tile_source,
        tile_target,
        tile_relation,
        tile_source,
        tile_target,
        type_bias,
        node_type.reshape(blocks, block),
        features.reshape(blocks, block, width),
        rel_weight,
        self_weight,
        tile_coef,
    )
    updated = pl.pallas_call(
        tile_kernel,
        out_shape=jax.ShapeDtypeStruct((blocks, block, width), kind),
        in_specs=[smem] * 3 + [anywhere] * 4,
        out_specs=anywhere,
        scratch_shapes=[
            pltpu.VMEM((block, block), kind),
            pltpu.VMEM((shards, block, width), kind),
            pltpu.VMEM((shards, width, width), kind),
            pltpu.VMEM((blocks, block, width), jnp.float32),
            pltpu.VMEM((blocks, block, width), kind),
            pltpu.VMEM((blocks, block, width), kind),
            pltpu.SMEM((groups,), jnp.int32),
            dma((2 * blocks + 3,)),
        ],
        compiler_params=pltpu.CompilerParams(vmem_limit_bytes=VMEM),
        name="tiles",
    )(tile_source, tile_target, tile_relation, tile_coef, pre, received, weights)
    return updated.reshape(rows, width)


def solution(mesh):
    placed = (
        P("graph", "feat"),
        P(None, "feat", None),
        P("feat", None),
        P(None, "feat"),
        P("graph"),
        P("graph", None, None),
        P("graph", None),
        P("graph", None),
        P("graph", None),
        P("graph", None),
        P("graph", None),
    )
    groups, shards = mesh.shape["graph"], mesh.shape["feat"]
    return jax.shard_map(
        functools.partial(per_device, groups, shards),
        mesh=mesh,
        in_specs=placed,
        out_specs=P("graph", "feat"),
        check_vma=False,
    )
```

time: 65.5 us -> 61.6 us (0.940)
  the two profiles are of different devices: /device:TPU:23 before, /device:TPU:6 now
where the time goes in v1:
time: 61.6 us; the launch traced here: 61.4 us
  Pallas kernels  61.4 us (100%)
    pallas_call x1, Pallas kernels, per_device(): pl.pallas_call(functools.partial(exchange_kernel, groups, shards, block),...  58.5 us
    pallas_call x1, Pallas kernels, per_device(): pl.pallas_call(tile_kernel, out_shape=jax.ShapeDtypeStruct((blocks, block...  2.86 us

profile of v1, /device:TPU:6, one launch (start us, length us, event | category | flops | bytes accessed | tf_op | source)
XLA Modules:
  0.0 61.4 jit_solution(7899803947012424251)
XLA Ops:
  0.0 58.5 %exchange.1 = (bf16[2,16,128,512]{3,2,1,0:T(8,128)(2,1)}, bf16[2,8,512,512]{3,2,1,0:T(8,128)(2,1)}, bf16[8,128,512]{2,1,0:T(8,128)(2,1)}) custom-call(s32[1,16]{1,0:T(1,128)} %send_block.1, s32[1,16]{1,0:T(1,128)} %send_live.1, s32[1,40]{1,0:T(1,128)} %tile_source.3, s32[1,40]{1,0:T(1,128)} %tile_target.3, s32[1,40]{1,0:T(1,128)} %tile_relation.3, ...), custom_call_target="tpu_custom_call" | custom-call | tf_op jit(solution)/shard_map/exchange/pallas_call | solution.py:487
  58.5 2.9 %tiles.1 = bf16[8,128,512]{2,1,0:T(8,128)(2,1)} custom-call(s32[1,40]{1,0:T(1,128)} %tile_source.3, s32[1,40]{1,0:T(1,128)} %tile_target.3, s32[1,40]{1,0:T(1,128)} %tile_relation.3, bf16[40,128,128]{2,1,0:T(8,128)(2,1)} %coef_hbm.3, bf16[8,128,512]{2,1,0:T(8,128)(2,1)} %get-tuple-element.8.pre_hbm, bf16[2,16,128,512]{3,2,1,0:T(8,128)(2,1)} %get-tuple-element.9.received, ...), custom_call_target="tpu_custom_call" | custom-call | tf_op jit(solution)/shard_map/tiles/pallas_call | solution.py:539

commit v2 on v1

--- a/solution.py
+++ b/solution.py
@@ -23,15 +23,13 @@
     groups,
     shards,
     block,
-    send_block,
-    send_live,
-    tile_source,
-    tile_target,
-    tile_relation,
-    source_row,
-    target_row,
-    bias_ref,
-    type_ref,
+    send_block_hbm,
+    send_live_hbm,
+    source_hbm,
+    target_hbm,
+    relation_hbm,
+    bias_hbm,
+    type_hbm,
     x_hbm,
     rel_ref,
     self_ref,
@@ -51,6 +49,16 @@
     pre,
     plan_vmem,
     plan,
+    send_block,
+    send_live,
+    tile_source,
+    tile_target,
+    tile_relation,
+    source_row,
+    target_row,
+    bias_ref,
+    type_ref,
+    small_sem,
     send_sem,
     recv_sem,
     pass_send,
@@ -92,50 +100,32 @@
         self_ref.at[:, columns(mine)], w_all.at[mine, relations], local_sem.at[1]
     )
     coef_copy = pltpu.make_async_copy(coef_hbm, coef, local_sem.at[4])
+    smalls = [
+        pltpu.make_async_copy(src, dst, small_sem.at[i])
+        for i, (src, dst) in enumerate(
+            (
+                (send_block_hbm, send_block),
+                (send_live_hbm, send_live),
+                (source_hbm, source_row),
+                (target_hbm, target_row),
+                (source_hbm, tile_source),
+                (target_hbm, tile_target),
+                (relation_hbm, tile_relation),
+                (bias_hbm, bias_ref),
+                (type_hbm, type_ref),
+            )
+        )
+    ]
     x_copy.start()
+    for copy in smalls:
+        copy.start()
+    smalls[0].wait()
+    smalls[1].wait()
+    x_copy.wait()
     own_rel.start()
     own_self.start()
     coef_copy.start()
-    x_copy.wait()
-
-    def gather(q, carry):
-        picked = x_own[send_block[0, q]].astype(jnp.float32)
-        outgoing[q] = (picked * send_live[0, q].astype(jnp.float32)).astype(outgoing.dtype)
-        return carry
-
-    lax.fori_loop(0, groups, gather, 0)
-
-    def iota(shape, axis):
-        return lax.broadcasted_iota(jnp.int32, shape, axis)
-
-    square = (tiles, tiles)
-    down, along = iota(square, 0), iota(square, 1)
-
-    def column(row):
-        return jnp.sum(
-            jnp.where(down == along, jnp.broadcast_to(row, square), 0), axis=1, keepdims=True
-        )
-
-    sources = column(source_row[...])
-    keys_row = jnp.where(source_row[...] < blocks, target_row[...], blocks)
-    keys = column(keys_row)
-    ahead = (keys_row < keys) | ((keys_row == keys) & (along < down))
-    rank = jnp.sum(ahead.astype(jnp.int32), axis=1, keepdims=True)
-    plan_vmem[0:1, 0:tiles] = jnp.sum(
-        jnp.where(rank == along, down, 0), axis=0, keepdims=True
-    )
-    wide = (tiles, groups)
-    plan_vmem[1:2, 0:groups] = jnp.min(
-        jnp.where(sources == blocks + iota(wide, 1), iota(wide, 0), tiles), axis=0, keepdims=True
-    )
-    each = (tiles, blocks)
-    plan_vmem[2:3, 0:blocks] = jnp.sum(
-        (keys <= iota(each, 1)).astype(jnp.int32), axis=0, keepdims=True
-    )
-    plan_vmem[3:4, 0:blocks] = jnp.sum(
-        (keys == iota(each, 1)).astype(jnp.int32), axis=0, keepdims=True
-    )
-    plan_copy = pltpu.make_async_copy(plan_vmem, plan, local_sem.at[5])
+
     with jax.named_scope("barrier"):
         pl.semaphore_wait(barrier, groups - 1 + shards - 1)
 
@@ -153,12 +143,22 @@
     half = groups // 2
     inner = (me // half + me // max(half // 2, 1)) % 2
 
+    def turn(i):
+        return 1 + (i + inner * (half - 1)) % (groups - 1)
+
+    def gather(i):
+        q = partner(me, turn(i), groups)
+        picked = x_own[send_block[0, q]].astype(jnp.float32)
+        outgoing[q] = (picked * send_live[0, q].astype(jnp.float32)).astype(outgoing.dtype)
+
     def send(i, carry):
-        boundary(1 + (i + inner * (half - 1)) % (groups - 1)).start()
+        gather(i + 1)
+        boundary(turn(i)).start()
         return carry
 
-    lax.fori_loop(0, groups - 1, send, 0)
-    plan_copy.start()
+    gather(0)
+    lax.fori_loop(0, groups - 2, send, 0)
+    boundary(turn(groups - 2)).start()
 
     def side(e):
         peer = (mine + e) % shards
@@ -182,6 +182,41 @@
     sides = [copy for e in range(1, shards) for copy in side(e)]
     for copy in sides:
         copy.start()
+    for copy in smalls[2:]:
+        copy.wait()
+
+    def iota(shape, axis):
+        return lax.broadcasted_iota(jnp.int32, shape, axis)
+
+    square = (tiles, tiles)
+    down, along = iota(square, 0), iota(square, 1)
+
+    def column(row):
+        return jnp.sum(
+            jnp.where(down == along, jnp.broadcast_to(row, square), 0), axis=1, keepdims=True
+        )
+
+    sources = column(source_row[...])
+    keys_row = jnp.where(source_row[...] < blocks, target_row[...], blocks)
+    keys = column(keys_row)
+    ahead = (keys_row < keys) | ((keys_row == keys) & (along < down))
+    rank = jnp.sum(ahead.astype(jnp.int32), axis=1, keepdims=True)
+    plan_vmem[0:1, 0:tiles] = jnp.sum(
+        jnp.where(rank == along, down, 0), axis=0, keepdims=True
+    )
+    wide = (tiles, groups)
+    plan_vmem[1:2, 0:groups] = jnp.min(
+        jnp.where(sources == blocks + iota(wide, 1), iota(wide, 0), tiles), axis=0, keepdims=True
+    )
+    each = (tiles, blocks)
+    plan_vmem[2:3, 0:blocks] = jnp.sum(
+        (keys <= iota(each, 1)).astype(jnp.int32), axis=0, keepdims=True
+    )
+    plan_vmem[3:4, 0:blocks] = jnp.sum(
+        (keys == iota(each, 1)).astype(jnp.int32), axis=0, keepdims=True
+    )
+    plan_copy = pltpu.make_async_copy(plan_vmem, plan, local_sem.at[5])
+    plan_copy.start()
     own_rel.wait()
     own_self.wait()
     with jax.named_scope("sides"):
@@ -319,20 +354,21 @@
             s_vmem[i] = s_vmem[i] + jnp.where(target == i, result, 0.0)
         return carry
 
-    late = max(groups // 4, 1)
+    ready = max(3 * groups // 4, 1)
 
     def serve(step, carry):
         arrived(step, carry)
-        return merge(step, carry)
+        return merge(step - 1, carry)
 
     with jax.named_scope("arrive"):
-        lax.fori_loop(1, groups - late, arrived, 0)
+        lax.fori_loop(1, ready, arrived, 0)
     with jax.named_scope("merge"):
-        lax.fori_loop(1, groups - late, merge, 0)
+        lax.fori_loop(1, ready - 1, merge, 0)
     with jax.named_scope("serve"):
-        lax.fori_loop(max(groups - late, 1), groups - 1, serve, 0)
+        lax.fori_loop(ready, groups - 1, serve, 0)
     with jax.named_scope("last"):
         arrived(groups - 1, 0)
+        merge(groups - 2, 0)
     with jax.named_scope("lastmv"):
         result, target = moved(groups - 1)
         outs = []
@@ -491,7 +527,7 @@
             jax.ShapeDtypeStruct((shards, relations, width, width), kind),
             jax.ShapeDtypeStruct((blocks, block, width), kind),
         ),
-        in_specs=[smem] * 5 + [vmem] * 4 + [anywhere] * 4,
+        in_specs=[anywhere] * 11,
         out_specs=(anywhere,) * 3,
         scratch_shapes=[
             pltpu.VMEM((groups, block, width), kind),
@@ -506,6 +542,16 @@
             pltpu.VMEM((blocks, block, width), kind),
             pltpu.VMEM((8, lanes), jnp.int32),
             pltpu.SMEM((8, lanes), jnp.int32),
+            pltpu.SMEM(send_block.shape, jnp.int32),
+            pltpu.SMEM(send_block.shape, jnp.int32),
+            pltpu.SMEM(tile_source.shape, jnp.int32),
+            pltpu.SMEM(tile_source.shape, jnp.int32),
+            pltpu.SMEM(tile_source.shape, jnp.int32),
+            pltpu.VMEM(tile_source.shape, jnp.int32),
+            pltpu.VMEM(tile_source.shape, jnp.int32),
+            pltpu.VMEM(type_bias.shape, jnp.float32),
+            pltpu.VMEM((blocks, block), jnp.int32),
+            dma((9,)),
             dma((groups,)),
             dma((groups,)),
             dma((max(shards - 1, 1), groups)),
@@ -527,8 +573,6 @@
         tile_source,
         tile_target,
         tile_relation,
-        tile_source,
-        tile_target,
         type_bias,
         node_type.reshape(blocks, block),
         features.reshape(blocks, block, width),

time: 61.6 us -> 58.1 us (0.943)
  the two profiles are of different devices: /device:TPU:6 before, /device:TPU:9 now
where the time goes in v2:
time: 58.1 us; the launch traced here: 57.9 us
  Pallas kernels  57.9 us (100%)
    pallas_call x1, Pallas kernels, per_device(): pl.pallas_call(functools.partial(exchange_kernel, groups, shards, block),...  55 us
    pallas_call x1, Pallas kernels, per_device(): pl.pallas_call(tile_kernel, out_shape=jax.ShapeDtypeStruct((blocks, block...  2.86 us

profile of v2, /device:TPU:9, one launch (start us, length us, event | category | flops | bytes accessed | tf_op | source)
XLA Modules:
  0.0 57.9 jit_solution(15196052492179179249)
XLA Ops:
  0.0 55.0 %exchange.1 = (bf16[2,16,128,512]{3,2,1,0:T(8,128)(2,1)}, bf16[2,8,512,512]{3,2,1,0:T(8,128)(2,1)}, bf16[8,128,512]{2,1,0:T(8,128)(2,1)}) custom-call(s32[1,16]{1,0:T(1,128)} %send_block_hbm.1, s32[1,16]{1,0:T(1,128)} %send_live_hbm.1, s32[1,40]{1,0:T(1,128)} %tile_source.1, s32[1,40]{1,0:T(1,128)} %tile_target.1, s32[1,40]{1,0:T(1,128)} %tile_relation.1, ...), custom_call_target="tpu_custom_call" | custom-call | tf_op jit(solution)/shard_map/exchange/pallas_call | solution.py:523
  55.1 2.9 %tiles.1 = bf16[8,128,512]{2,1,0:T(8,128)(2,1)} custom-call(s32[1,40]{1,0:T(1,128)} %tile_source.1, s32[1,40]{1,0:T(1,128)} %tile_target.1, s32[1,40]{1,0:T(1,128)} %tile_relation.1, bf16[40,128,128]{2,1,0:T(8,128)(2,1)} %coef_hbm.3, bf16[8,128,512]{2,1,0:T(8,128)(2,1)} %get-tuple-element.8.pre_hbm, bf16[2,16,128,512]{3,2,1,0:T(8,128)(2,1)} %get-tuple-element.9.received, ...), custom_call_target="tpu_custom_call" | custom-call | tf_op jit(solution)/shard_map/tiles/pallas_call | solution.py:583

commit v3 on v2

--- a/solution.py
+++ b/solution.py
@@ -354,21 +354,20 @@
             s_vmem[i] = s_vmem[i] + jnp.where(target == i, result, 0.0)
         return carry
 
-    ready = max(3 * groups // 4, 1)
+    late = max(groups // 4, 1)
 
     def serve(step, carry):
         arrived(step, carry)
-        return merge(step - 1, carry)
+        return merge(step, carry)
 
     with jax.named_scope("arrive"):
-        lax.fori_loop(1, ready, arrived, 0)
+        lax.fori_loop(1, groups - late, arrived, 0)
     with jax.named_scope("merge"):
-        lax.fori_loop(1, ready - 1, merge, 0)
+        lax.fori_loop(1, groups - late, merge, 0)
     with jax.named_scope("serve"):
-        lax.fori_loop(ready, groups - 1, serve, 0)
+        lax.fori_loop(max(groups - late, 1), groups - 1, serve, 0)
     with jax.named_scope("last"):
         arrived(groups - 1, 0)
-        merge(groups - 2, 0)
     with jax.named_scope("lastmv"):
         result, target = moved(groups - 1)
         outs = []
@@ -392,6 +391,420 @@
         w_copy.wait()
         for copy in outs:
             copy.wait()
+
+
+def relay_kernel(
+    groups,
+    shards,
+    block,
+    send_block_hbm,
+    send_live_hbm,
+    source_hbm,
+    target_hbm,
+    relation_hbm,
+    bias_hbm,
+    type_hbm,
+    x_hbm,
+    rel_ref,
+    self_ref,
+    coef_hbm,
+    pre_out,
+    flag_out,
+    outgoing,
+    x_own,
+    x_far,
+    w_all,
+    s_vmem,
+    coef,
+    sums,
+    landed,
+    far,
+    list_out,
+    list_in,
+    relayed,
+    table_out,
+    table_in,
+    table,
+    flags,
+    flag_vmem,
+    plan_vmem,
+    plan,
+    send_block,
+    send_live,
+    tile_source,
+    tile_target,
+    tile_relation,
+    source_row,
+    target_row,
+    bias_ref,
+    type_ref,
+    small_sem,
+    send_sem,
+    recv_sem,
+    pass_send,
+    pass_recv,
+    side_send,
+    side_recv,
+    local_sem,
+    list_send,
+    list_recv,
+    relay_send,
+    flag_send,
+    flag_recv,
+    table_sem,
+):
+    me, mine = lax.axis_index("graph"), lax.axis_index("feat")
+    blocks, _, width = x_own.shape
+    relations = rel_ref.shape[0]
+    tiles = coef.shape[0]
+
+    def columns(shard):
+        return pl.ds(pl.multiple_of(shard * width, width), width)
+
+    barrier = pltpu.get_barrier_semaphore()
+
+    def greet(step, carry):
+        pl.semaphore_signal(
+            barrier, inc=1, device_id=(partner(me, step, groups), mine), device_id_type=MESH
+        )
+        return carry
+
+    lax.fori_loop(1, groups, greet, 0)
+    for e in range(1, shards):
+        pl.semaphore_signal(
+            barrier, inc=1, device_id=(me, (mine + e) % shards), device_id_type=MESH
+        )
+
+    x_copy = pltpu.make_async_copy(x_hbm, x_own, local_sem.at[3])
+    own_rel = pltpu.make_async_copy(
+        rel_ref.at[:, :, columns(mine)], w_all.at[mine, pl.ds(0, relations)], local_sem.at[0]
+    )
+    own_self = pltpu.make_async_copy(
+        self_ref.at[:, columns(mine)], w_all.at[mine, relations], local_sem.at[1]
+    )
+    coef_copy = pltpu.make_async_copy(coef_hbm, coef, local_sem.at[4])
+    smalls = [
+        pltpu.make_async_copy(src, dst, small_sem.at[i])
+        for i, (src, dst) in enumerate(
+            (
+                (send_block_hbm, send_block),
+                (send_live_hbm, send_live),
+                (source_hbm, source_row),
+                (target_hbm, target_row),
+                (source_hbm, tile_source),
+                (target_hbm, tile_target),
+                (relation_hbm, tile_relation),
+                (bias_hbm, bias_ref),
+                (type_hbm, type_ref),
+            )
+        )
+    ]
+    x_copy.start()
+    for copy in smalls:
+        copy.start()
+    smalls[0].wait()
+    smalls[1].wait()
+    x_copy.wait()
+    own_rel.start()
+    own_self.start()
+    coef_copy.start()
+
+    def boundary(step):
+        other = partner(me, step, groups)
+        return pltpu.make_async_remote_copy(
+            src_ref=outgoing.at[other],
+            dst_ref=landed.at[me],
+            send_sem=send_sem.at[step],
+            recv_sem=recv_sem.at[step],
+            device_id=(other, mine),
+            device_id_type=MESH,
+        )
+
+    plane = groups // 4
+    level = me // plane
+    middle = (level + level // 2) % 2
+    inner, outer = middle == 1, middle == 0
+
+    def gather(step, carry):
+        q = partner(me, step, groups)
+        picked = x_own[send_block[0, q]].astype(jnp.float32)
+        outgoing[q] = (picked * send_live[0, q].astype(jnp.float32)).astype(outgoing.dtype)
+        return carry
+
+    def send(step, carry):
+        boundary(step).start()
+        return carry
+
+    lax.fori_loop(1, groups, gather, 0)
+    smalls[2].wait()
+
+    def iota(shape, axis):
+        return lax.broadcasted_iota(jnp.int32, shape, axis)
+
+    square = (tiles, tiles)
+    down, along = iota(square, 0), iota(square, 1)
+
+    def column(row):
+        return jnp.sum(
+            jnp.where(down == along, jnp.broadcast_to(row, square), 0), axis=1, keepdims=True
+        )
+
+    sources = column(source_row[...])
+    wide = (tiles, groups)
+    first_row = jnp.min(
+        jnp.where(sources == blocks + iota(wide, 1), iota(wide, 0), tiles), axis=0, keepdims=True
+    )
+    plan_vmem[1:2, 0:groups] = first_row
+    named = (first_row < tiles).astype(jnp.int32)
+    repeats = jnp.sum(
+        (source_row[...] >= blocks).astype(jnp.int32), axis=1, keepdims=True
+    ) - jnp.sum(named, axis=1, keepdims=True)
+    flags[me] = jnp.broadcast_to(repeats, flags.shape[1:])
+
+    def flagged(step):
+        return pltpu.make_async_remote_copy(
+            src_ref=flags.at[me],
+            dst_ref=flags.at[me],
+            send_sem=flag_send.at[step],
+            recv_sem=flag_recv.at[step],
+            device_id=(partner(me, step, groups), mine),
+            device_id_type=MESH,
+        )
+
+    with jax.named_scope("barrier"):
+        pl.semaphore_wait(barrier, groups - 1 + shards - 1)
+
+    def tell(step, carry):
+        flagged(step).start()
+        return carry
+
+    lax.fori_loop(1, groups, tell, 0)
+    @pl.when(inner)
+    def _():
+        lax.fori_loop(2 * plane, groups, send, 0)
+
+    lax.fori_loop(1, 2 * plane, send, 0)
+
+    @pl.when(outer)
+    def _():
+        lax.fori_loop(2 * plane, groups, send, 0)
+
+    def side(e):
+        peer = (mine + e) % shards
+        pairs = (
+            (x_own, x_far.at[mine]),
+            (self_ref.at[:, columns(peer)], w_all.at[mine, relations]),
+            (rel_ref.at[:, :, columns(peer)], w_all.at[mine, pl.ds(0, relations)]),
+        )
+        return [
+            pltpu.make_async_remote_copy(
+                src_ref=src,
+                dst_ref=dst,
+                send_sem=side_send.at[e - 1, i],
+                recv_sem=side_recv.at[e - 1, i],
+                device_id=(me, peer),
+                device_id_type=MESH,
+            )
+            for i, (src, dst) in enumerate(pairs)
+        ]
+
+    sides = [copy for e in range(1, shards) for copy in side(e)]
+    for copy in sides:
+        copy.start()
+    for copy in smalls[3:]:
+        copy.wait()
+
+    keys_row = jnp.where(source_row[...] < blocks, target_row[...], blocks)
+    keys = column(keys_row)
+    ahead = (keys_row < keys) | ((keys_row == keys) & (along < down))
+    rank = jnp.sum(ahead.astype(jnp.int32), axis=1, keepdims=True)
+    plan_vmem[0:1, 0:tiles] = jnp.sum(
+        jnp.where(rank == along, down, 0), axis=0, keepdims=True
+    )
+    each = (tiles, blocks)
+    plan_vmem[2:3, 0:blocks] = jnp.sum(
+        (keys <= iota(each, 1)).astype(jnp.int32), axis=0, keepdims=True
+    )
+    plan_vmem[3:4, 0:blocks] = jnp.sum(
+        (keys == iota(each, 1)).astype(jnp.int32), axis=0, keepdims=True
+    )
+    plan_copy = pltpu.make_async_copy(plan_vmem, plan, local_sem.at[5])
+    plan_copy.start()
+    own_rel.wait()
+    own_self.wait()
+    with jax.named_scope("sides"):
+        for copy in sides:
+            copy.wait()
+    chunk = 2
+
+    def full_dot(start, relation):
+        at = pl.ds(start, chunk)
+        total = jnp.dot(
+            x_own[at].reshape(chunk * block, width),
+            w_all[mine, relation],
+            preferred_element_type=jnp.float32,
+        )
+        for e in range(1, shards):
+            peer = (mine + e) % shards
+            total = total + jnp.dot(
+                x_far[peer, at].reshape(chunk * block, width),
+                w_all[peer, relation],
+                preferred_element_type=jnp.float32,
+            )
+        return total.reshape(chunk, block, width)
+
+    def own_part(i, carry):
+        s_vmem[pl.ds(i * chunk, chunk)] = full_dot(i * chunk, relations)
+        return carry
+
+    with jax.named_scope("self"):
+        lax.fori_loop(0, blocks // chunk, own_part, 0)
+
+    coef_copy.wait()
+    plan_copy.wait()
+    stride = 4 if tiles % 4 == 0 else 1
+
+    def local(i, carry):
+        terms = []
+        for j in range(stride):
+            t = plan[0, i * stride + j]
+            relation = tile_relation[0, t]
+            source = jnp.minimum(tile_source[0, t], blocks - 1)
+            value = jnp.dot(
+                x_own[source], w_all[mine, relation], preferred_element_type=jnp.float32
+            )
+            for e in range(1, shards):
+                peer = (mine + e) % shards
+                value = value + jnp.dot(
+                    x_far[peer, source], w_all[peer, relation], preferred_element_type=jnp.float32
+                )
+            terms.append((t, value.astype(coef.dtype)))
+        for j, (t, value) in enumerate(terms):
+            at = i * stride + j
+            before = plan[0, jnp.maximum(at - 1, 0)]
+            joins = (tile_target[0, t] == tile_target[0, before]) & (at > 0)
+            term = jnp.dot(coef[t], value, preferred_element_type=jnp.float32)
+            sums[at] = term + jnp.where(joins, sums[jnp.maximum(at - 1, 0)], 0.0)
+        return carry
+
+    ahead_of_relay = 7 * tiles // (10 * stride)
+    with jax.named_scope("local"):
+        lax.fori_loop(0, ahead_of_relay, local, 0)
+
+    with jax.named_scope("local2"):
+        lax.fori_loop(ahead_of_relay, tiles // stride, local, 0)
+
+    with jax.named_scope("base"):
+        for i in range(blocks):
+            kinds = jnp.transpose(jnp.broadcast_to(type_ref[i : i + 1, :], (block, block)))
+            kinds = jnp.concatenate([kinds] * (width // block), axis=1)
+            total = s_vmem[i]
+            for kind in range(bias_ref.shape[0]):
+                total = total + jnp.where(kinds == kind, bias_ref[kind : kind + 1, :], 0.0)
+            last = jnp.maximum(plan[2, i] - 1, 0)
+            s_vmem[i] = total + jnp.where(plan[3, i] > 0, sums[last], 0.0)
+
+    def forward(step, e):
+        other = partner(me, step, groups)
+        return pltpu.make_async_remote_copy(
+            src_ref=landed.at[other],
+            dst_ref=far.at[mine, other],
+            send_sem=pass_send.at[e - 1, step],
+            recv_sem=pass_recv.at[e - 1, step],
+            device_id=(me, (mine + e) % shards),
+            device_id_type=MESH,
+        )
+
+    def order(i):
+        return i
+
+    def arrived(i, carry):
+        step = order(i)
+
+        boundary(step).wait_recv()
+        for e in range(1, shards):
+            forward(step, e).start()
+        return carry
+
+    def moved(i):
+        step = order(i)
+        other = partner(me, step, groups)
+        found = plan[1, other]
+        t = jnp.minimum(found, tiles - 1)
+        relation = tile_relation[0, t]
+        value = jnp.dot(
+            landed[other], w_all[mine, relation], preferred_element_type=jnp.float32
+        )
+        for e in range(1, shards):
+            origin = (mine + shards - e) % shards
+            pltpu.make_async_remote_copy(
+                src_ref=far.at[origin, other],
+                dst_ref=far.at[origin, other],
+                send_sem=pass_send.at[e - 1, step],
+                recv_sem=pass_recv.at[e - 1, step],
+                device_id=(me, (mine + e) % shards),
+                device_id_type=MESH,
+            ).wait_recv()
+            value = value + jnp.dot(
+                far[origin, other], w_all[origin, relation], preferred_element_type=jnp.float32
+            )
+        value = value.astype(coef.dtype)
+        result = jnp.dot(coef[t], value, preferred_element_type=jnp.float32)
+        return result, jnp.where(found < tiles, tile_target[0, t], -1)
+
+    def merge(step, carry):
+        result, target = moved(step)
+        for i in range(blocks):
+            s_vmem[i] = s_vmem[i] + jnp.where(target == i, result, 0.0)
+        return carry
+
+    def serve(i, carry):
+        arrived(i, carry)
+        return merge(i - 1, carry)
+
+    def told(step, carry):
+        flagged(step).wait()
+        return carry
+
+    flag_copy = pltpu.make_async_copy(flag_vmem, flag_out, table_sem.at[1])
+    with jax.named_scope("arrive"):
+        lax.fori_loop(1, groups, told, 0)
+        flag_vmem[...] = jnp.max(flags[...], axis=0)
+        lax.fori_loop(1, 2 * plane, arrived, 0)
+    with jax.named_scope("merge"):
+        lax.fori_loop(1, 2 * plane - 1, merge, 0)
+    flag_copy.start()
+    with jax.named_scope("serve"):
+        lax.fori_loop(2 * plane, groups - 1, serve, 0)
+    with jax.named_scope("last"):
+        arrived(groups - 1, 0)
+    with jax.named_scope("lastm"):
+        merge(groups - 2, 0)
+    with jax.named_scope("lastmv"):
+        result, target = moved(groups - 1)
+        for i in range(blocks):
+            value = s_vmem[i] + jnp.where(target == i, result, 0.0)
+            pre_out[i] = jnp.maximum(value, 0.0).astype(pre_out.dtype)
+
+    def finish(step, carry):
+        for e in range(1, shards):
+            forward(step, e).wait_send()
+        return carry
+
+    def finish_send(step, carry):
+        boundary(step).wait_send()
+        return carry
+
+    with jax.named_scope("finish"):
+        lax.fori_loop(1, groups, finish, 0)
+        lax.fori_loop(1, groups, finish_send, 0)
+        flag_copy.wait()
+
+
+def store_kernel(x_ref, out_hbm, sem):
+    copy = pltpu.make_async_copy(x_ref, out_hbm, sem)
+    copy.start()
+    copy.wait()
 
 
 def tile_kernel(
@@ -517,18 +930,103 @@
     smem = pl.BlockSpec(memory_space=pltpu.SMEM)
     vmem = pl.BlockSpec(memory_space=pltpu.VMEM)
     anywhere = pl.BlockSpec(memory_space=pl.ANY)
+    hbm = pl.BlockSpec(memory_space=pltpu.HBM)
     dma = pltpu.SemaphoreType.DMA
     blocks = rows // block
     lanes = 128 * pl.cdiv(max(tiles, groups, blocks), 128)
-    received, weights, pre = pl.pallas_call(
-        functools.partial(exchange_kernel, groups, shards, block),
+    plane = groups // 4
+    capacity = 3 * blocks // 4 if 2 * plane <= blocks else blocks
+    wide = (1, 128)
+    operands = (
+        send_block,
+        send_live,
+        tile_source,
+        tile_target,
+        tile_relation,
+        type_bias,
+        node_type.reshape(blocks, block),
+        features.reshape(blocks, block, width),
+        rel_weight,
+        self_weight,
+        tile_coef,
+    )
+    def dense():
+        received, weights, pre = pl.pallas_call(
+            functools.partial(exchange_kernel, groups, shards, block),
+            out_shape=(
+                jax.ShapeDtypeStruct((shards, groups, block, width), kind),
+                jax.ShapeDtypeStruct((shards, relations, width, width), kind),
+                jax.ShapeDtypeStruct((blocks, block, width), kind),
+            ),
+            in_specs=[anywhere] * 11,
+            out_specs=(anywhere,) * 3,
+            scratch_shapes=[
+                pltpu.VMEM((groups, block, width), kind),
+                pltpu.VMEM((blocks, block, width), kind),
+                pltpu.VMEM((shards, blocks, block, width), kind),
+                pltpu.VMEM((shards, relations + 1, width, width), kind),
+                pltpu.VMEM((blocks, block, width), jnp.float32),
+                pltpu.VMEM((tiles, block, block), kind),
+                pltpu.VMEM((tiles, block, width), jnp.float32),
+                pltpu.VMEM((groups, block, width), kind),
+                pltpu.VMEM((shards, groups, block, width), kind),
+                pltpu.VMEM((blocks, block, width), kind),
+                pltpu.VMEM((8, lanes), jnp.int32),
+                pltpu.SMEM((8, lanes), jnp.int32),
+                pltpu.SMEM(send_block.shape, jnp.int32),
+                pltpu.SMEM(send_block.shape, jnp.int32),
+                pltpu.SMEM(tile_source.shape, jnp.int32),
+                pltpu.SMEM(tile_source.shape, jnp.int32),
+                pltpu.SMEM(tile_source.shape, jnp.int32),
+                pltpu.VMEM(tile_source.shape, jnp.int32),
+                pltpu.VMEM(tile_source.shape, jnp.int32),
+                pltpu.VMEM(type_bias.shape, jnp.float32),
+                pltpu.VMEM((blocks, block), jnp.int32),
+                dma((9,)),
+                dma((groups,)),
+                dma((groups,)),
+                dma((max(shards - 1, 1), groups)),
+                dma((max(shards - 1, 1), groups)),
+                dma((max(shards - 1, 1), 3)),
+                dma((max(shards - 1, 1), 3)),
+                dma((6,)),
+                dma((groups,)),
+                dma((max(shards - 1, 1), groups)),
+                dma((blocks,)),
+            ],
+            compiler_params=pltpu.CompilerParams(
+                collective_id=1, has_side_effects=True, vmem_limit_bytes=VMEM
+            ),
+            name="exchange",
+        )(*operands)
+        updated = pl.pallas_call(
+            tile_kernel,
+            out_shape=jax.ShapeDtypeStruct((blocks, block, width), kind),
+            in_specs=[smem] * 3 + [anywhere] * 4,
+            out_specs=anywhere,
+            scratch_shapes=[
+                pltpu.VMEM((block, block), kind),
+                pltpu.VMEM((shards, block, width), kind),
+                pltpu.VMEM((shards, width, width), kind),
+                pltpu.VMEM((blocks, block, width), jnp.float32),
+                pltpu.VMEM((blocks, block, width), kind),
+                pltpu.VMEM((blocks, block, width), kind),
+                pltpu.SMEM((groups,), jnp.int32),
+                dma((2 * blocks + 3,)),
+            ],
+            compiler_params=pltpu.CompilerParams(vmem_limit_bytes=VMEM),
+            name="tiles",
+        )(tile_source, tile_target, tile_relation, tile_coef, pre, received, weights)
+        return updated
+
+    result, flag = pl.pallas_call(
+        functools.partial(relay_kernel, groups, shards, block),
         out_shape=(
-            jax.ShapeDtypeStruct((shards, groups, block, width), kind),
-            jax.ShapeDtypeStruct((shards, relations, width, width), kind),
             jax.ShapeDtypeStruct((blocks, block, width), kind),
+            jax.ShapeDtypeStruct((1, 128), jnp.int32),
         ),
-        in_specs=[anywhere] * 11,
-        out_specs=(anywhere,) * 3,
+        in_specs=[hbm] * 11,
+        out_specs=(vmem, hbm),
         scratch_shapes=[
             pltpu.VMEM((groups, block, width), kind),
             pltpu.VMEM((blocks, block, width), kind),
@@ -539,7 +1037,14 @@
             pltpu.VMEM((tiles, block, width), jnp.float32),
             pltpu.VMEM((groups, block, width), kind),
             pltpu.VMEM((shards, groups, block, width), kind),
-            pltpu.VMEM((blocks, block, width), kind),
+            pltpu.VMEM((capacity, block, width), kind),
+            pltpu.VMEM((capacity, block, width), kind),
+            pltpu.VMEM((2 * plane, block, width), kind),
+            pltpu.VMEM((2 * plane, 128), jnp.int32),
+            pltpu.VMEM((2 * plane, 128), jnp.int32),
+            pltpu.SMEM((2 * plane, 128), jnp.int32),
+            pltpu.VMEM((groups, 1, 128), jnp.int32),
+            pltpu.VMEM((1, 128), jnp.int32),
             pltpu.VMEM((8, lanes), jnp.int32),
             pltpu.SMEM((8, lanes), jnp.int32),
             pltpu.SMEM(send_block.shape, jnp.int32),
@@ -559,45 +1064,31 @@
             dma((max(shards - 1, 1), 3)),
             dma((max(shards - 1, 1), 3)),
             dma((6,)),
+            dma((capacity + 1,)),
+            dma((capacity + 1,)),
+            dma((2 * plane,)),
             dma((groups,)),
-            dma((max(shards - 1, 1), groups)),
-            dma((blocks,)),
+            dma((groups,)),
+            dma((2,)),
         ],
         compiler_params=pltpu.CompilerParams(
-            collective_id=0, has_side_effects=True, vmem_limit_bytes=VMEM
+            collective_id=0, has_side_effects=True, vmem_limit_bytes=56 << 20
         ),
-        name="exchange",
-    )(
-        send_block,
-        send_live,
-        tile_source,
-        tile_target,
-        tile_relation,
-        type_bias,
-        node_type.reshape(blocks, block),
-        features.reshape(blocks, block, width),
-        rel_weight,
-        self_weight,
-        tile_coef,
-    )
-    updated = pl.pallas_call(
-        tile_kernel,
-        out_shape=jax.ShapeDtypeStruct((blocks, block, width), kind),
-        in_specs=[smem] * 3 + [anywhere] * 4,
-        out_specs=anywhere,
-        scratch_shapes=[
-            pltpu.VMEM((block, block), kind),
-            pltpu.VMEM((shards, block, width), kind),
-            pltpu.VMEM((shards, width, width), kind),
-            pltpu.VMEM((blocks, block, width), jnp.float32),
-            pltpu.VMEM((blocks, block, width), kind),
-            pltpu.VMEM((blocks, block, width), kind),
-            pltpu.SMEM((groups,), jnp.int32),
-            dma((2 * blocks + 3,)),
-        ],
-        compiler_params=pltpu.CompilerParams(vmem_limit_bytes=VMEM),
-        name="tiles",
-    )(tile_source, tile_target, tile_relation, tile_coef, pre, received, weights)
+        name="relay",
+    )(*operands)
+
+    def store():
+        return pl.pallas_call(
+            store_kernel,
+            out_shape=jax.ShapeDtypeStruct((blocks, block, width), kind),
+            in_specs=[vmem],
+            out_specs=hbm,
+            scratch_shapes=[dma(())],
+            compiler_params=pltpu.CompilerParams(vmem_limit_bytes=2 << 20),
+            name="store",
+        )(result)
+
+    updated = lax.cond(flag[0, 0] > 0, dense, store)
     return updated.reshape(rows, width)
 
 

time: 58.1 us -> 57.8 us (level)
  Pallas kernels: 57.9 us -> 57 us
  between operations: 0.01 us -> 0.62 us
    pallas_call x2, Pallas kernels: 57.9 us -> 57 us  [the longest x1 56 us: per_device(): pl.pallas_call(functools.partial(relay_kernel, groups, shards, block), ou...]
where the time goes in v3:
time: 57.8 us; the launch traced here: 57.6 us
  Pallas kernels  57 us (99%)
  between operations  0.62 us (1%)
    pallas_call x1, Pallas kernels, per_device(): pl.pallas_call(functools.partial(relay_kernel, groups, shards, block), ou...  56 us

profile of v3, /device:TPU:9, one launch (start us, length us, event | category | flops | bytes accessed | tf_op | source)
XLA Modules:
  0.0 57.6 jit_solution(3787209737379478542)
XLA Ops:
  0.0 56.0 %relay.1 = (bf16[8,128,512]{2,1,0:T(8,128)(2,1)S(1)}, s32[1,128]{1,0:T(1,128)}) custom-call(s32[1,16]{1,0:T(1,128)} %send_block_hbm.1, s32[1,16]{1,0:T(1,128)} %send_live_hbm.1, s32[1,40]{1,0:T(1,128)} %source_hbm.1, s32[1,40]{1,0:T(1,128)} %target_hbm.1, s32[1,40]{1,0:T(1,128)} %relation_hbm.1, f32[4,512]{1,0:T(4,128)} %bias_hbm.1, s32[8,128]{1,0:T(8,128)} %bitcast.8, ...), custom_call_target="tpu_custom_call" | custom-call | tf_op jit(solution)/shard_map/relay/pallas_call | solution.py:1022
  56.6 1.0 %conditional.1 = (bf16[1024,512]{1,0:T(8,128)(2,1)}) conditional(s32[]{:T(128)} %bitcast.4, bf16[8,128,512]{2,1,0:T(8,128)(2,1)S(1)} %get-tuple-element.49, (s32[1,16]{1,0:T(1,128)}, s32[1,16]{1,0:T(1,128)}, s32[1,40]{1,0:T(1,128)}, s32[1,40]{1,0:T(1,128)}, s32[1,40]{1,0:T(1,128)}, /*index=5*/f32[4,512]{1,0:T(4,128)}, s32[8,128]{1,0:T(8,128)}, ...), branch_computations={%region_0.0_spmd, %region_1.0_spmd} | conditional | bytes 8 | solution.py:1091
  56.6 1.0 %store.1 = bf16[8,128,512]{2,1,0:T(8,128)(2,1)} custom-call(bf16[8,128,512]{2,1,0:T(8,128)(2,1)S(1)} %x_ref), custom_call_target="tpu_custom_call" | custom-call | tf_op jit(solution)/shard_map/cond/branch_0_fun/store/pallas_call | solution.py:1081
